TPU v7x, 32 devices: a whole 2x2x4 slice. The times are simulated.
32 devices in a mesh: data: 2 (over x), col: 4 (over z), row: 4 (over y, core).
Axes of the slice: x: 2, y: 2, z: 4, core: 2. Of those that a mesh axis runs over, the one named last changes fastest.
Arguments:
- pair_rep: bfloat16 [768, 384, 64], P(('data', 'row'), 'col'), parts along dimension 0
- res_mask: int32 [768], P('data'), parts along dimension 0
- ln_gamma: float32 [64], replicated
- ln_beta: float32 [64], replicated
- w_q: bfloat16 [64, 64], replicated
- w_k: bfloat16 [64, 64], replicated
- w_v: bfloat16 [64, 64], replicated
- w_b: bfloat16 [64, 4], replicated
- w_g: bfloat16 [64, 64], replicated
- w_o: bfloat16 [64, 64], replicated
Outputs:
- output: bfloat16 [768, 384, 64], P(('data', 'row'), 'col'), parts along dimension 0
There are 2 independent parts. A program takes and returns all parts, laid end to end along the dimension named above; an argument that names none is the same for every part.
All inputs are finite; a program needn't handle non-finite values.
Results may differ from a plain program's by a relative error of at most 0.00624027.
Values are sent between devices in bfloat16 or wider.
A program may use at most 1 GiB of HBM per device.

v0:
```python
import math
import jax
import jax.numpy as jnp
from jax import lax
from jax.sharding import PartitionSpec as P

LN_EPS = 1e-5
MASK_FILL = -1e9


def norm_and_project(pair_tile, ln_gamma, ln_beta, w_q, w_k, w_v, w_b, w_g):
    n_chan = pair_tile.shape[-1]
    heads = w_b.shape[1]
    head_dim = w_q.shape[1] // heads
    pair_f32 = pair_tile.astype(jnp.float32)
    mean = jnp.mean(pair_f32, axis=-1, keepdims=True)
    centred = pair_f32 - mean
    variance = jnp.mean(centred * centred, axis=-1, keepdims=True)
    normed = (centred * lax.rsqrt(variance + LN_EPS) * ln_gamma + ln_beta).astype(jnp.bfloat16)
    query = (jnp.einsum('ijc,chd->jhid', normed, w_q.reshape(n_chan, heads, head_dim), preferred_element_type=jnp.float32) * (1.0 / math.sqrt(head_dim))).astype(jnp.bfloat16)
    w_kv = jnp.stack([w_k.reshape(n_chan, heads, head_dim), w_v.reshape(n_chan, heads, head_dim)])
    kv_pair = jnp.einsum('ijc,echd->ejhid', normed, w_kv, preferred_element_type=jnp.float32).astype(jnp.bfloat16)
    gate = jax.nn.sigmoid(jnp.einsum('ijc,chd->jhid', normed, w_g.reshape(n_chan, heads, head_dim), preferred_element_type=jnp.float32))
    bias_tile = jnp.einsum('ijc,ch->ijh', normed, w_b, preferred_element_type=jnp.float32).astype(jnp.bfloat16)
    return pair_f32, query, kv_pair, gate, bias_tile


def bias_strip(bias_tile):
    full_cols = lax.all_gather(bias_tile, 'col', axis=1, tiled=True)
    own_rows = lax.all_to_all(full_cols, 'row', 1, 0, tiled=True)
    return jnp.transpose(own_rows, (2, 1, 0))


def attend_block(state, query, kv_blk, bias_blk, fill_blk):
    run_max, run_sum, out_acc = state
    logits = jnp.einsum('jhid,jhkd->jhik', query, kv_blk[0], preferred_element_type=jnp.float32) + bias_blk[None] + fill_blk
    new_max = jnp.maximum(run_max, jnp.max(logits, axis=-1))
    rescale = jnp.exp(run_max - new_max)
    p_exp = jnp.exp(logits - new_max[..., None])
    run_sum = run_sum * rescale + jnp.sum(p_exp, axis=-1)
    out_acc = out_acc * rescale[..., None] + jnp.einsum('jhik,jhkd->jhid', p_exp.astype(jnp.bfloat16), kv_blk[1], preferred_element_type=jnp.float32)
    return new_max, run_sum, out_acc


def finish(state, gate, pair_f32, w_o):
    run_max, run_sum, out_acc = state
    heads = gate.shape[1]
    head_dim = gate.shape[3]
    gated = (gate * (out_acc / run_sum[..., None])).astype(jnp.bfloat16)
    update = jnp.einsum('jhid,hdc->ijc', gated, w_o.reshape(heads, head_dim, w_o.shape[1]), preferred_element_type=jnp.float32)
    return (pair_f32 + update).astype(jnp.bfloat16)


def solution(mesh):
    rows = mesh.shape['row']
    next_hop = [(src_id, (src_id + 1) % rows) for src_id in range(rows)]

    def body(pair_tile, res_mask, ln_gamma, ln_beta, w_q, w_k, w_v, w_b, w_g, w_o):
        pair_f32, query, kv_pair, gate, bias_tile = norm_and_project(pair_tile, ln_gamma, ln_beta, w_q, w_k, w_v, w_b, w_g)
        strip = bias_strip(bias_tile)
        key_fill = jnp.where(res_mask > 0, 0.0, MASK_FILL).astype(jnp.float32)
        block = pair_tile.shape[0]
        my_row = lax.axis_index('row')

        def fold(step, state, kv_blk):
            key_lo = ((my_row - step) % rows) * block
            bias_blk = lax.dynamic_slice_in_dim(strip, key_lo, block, axis=2)
            fill_blk = lax.dynamic_slice_in_dim(key_fill, key_lo, block)
            return attend_block(state, query, kv_blk, bias_blk, fill_blk)

        stat_shape = query.shape[:3]
        state = (jnp.full(stat_shape, -jnp.inf, jnp.float32), jnp.zeros(stat_shape, jnp.float32), jnp.zeros(query.shape, jnp.float32))
        state = fold(0, state, kv_pair)

        def shift_step(step, carry):
            cur_state, kv_blk = carry
            kv_blk = lax.ppermute(kv_blk, 'row', next_hop)
            return fold(step, cur_state, kv_blk), kv_blk

        state, kv_last = lax.fori_loop(1, rows, shift_step, (state, kv_pair))
        return finish(state, gate, pair_f32, w_o)

    tile_spec = P(('data', 'row'), 'col', None)
    return jax.shard_map(body, mesh=mesh, in_specs=(tile_spec, P('data'), P(), P(), P(), P(), P(), P(), P(), P()), out_specs=tile_spec, check_vma=False)
```

profile of v0, /device:TPU:0, one launch (start us, length us, event | category | flops | bytes accessed | tf_op | source)
XLA Modules:
  0.0 342.0 jit_solution(2792890093256478573)
XLA Ops:
  0.0 4.5 %copy.62 = bf16[96,96,64]{0,2,1:T(8,128)(2,1)S(1)} copy(bf16[96,96,64]{1,2,0:T(8,128)(2,1)} %param.12) | data formatting | bytes 2359296 | tf_op args[0]
  6.6 16.3 %all_gather.3 = bf16[96,384,4]{0,2,1:T(4,128)(2,1)} all-gather(bf16[96,96,4]{0,2,1:T(4,128)(2,1)S(1)} %convolution_convert_fusion), channel_id=1, replica_groups=mesh['data'=2,'col'=4,'row'=4] {'col'}, dimensions={1}, use_global_device_ids=true | all-gather | bytes 368640 | tf_op jit(solution)/shard_map/all_gather | solution.py:29
  22.9 4.3 %all-to-all-start = ((bf16[96,384,4]{0,2,1:T(4,128)(2,1)}), bf16[96,384,4]{0,2,1:T(4,128)(2,1)}, u32[]{:S(2)}, u32[]{:S(2)}) async-start(bf16[96,384,4]{0,2,1:T(4,128)(2,1)} %all_gather.3), calls=%async_computation | async-start | bytes 786432 | tf_op jit(solution)/shard_map/all_to_all | solution.py:30
  27.9 1.8 fusion.45
  29.7 4.0 %copy.81 = bf16[96,96,64,1,1]{1,2,0,4,3:T(8,128)(2,1)} copy(bf16[96,96,64,1,1]{0,2,1,4,3:T(8,128)(2,1)S(1)} %fusion.44) | data formatting | bytes 2359296 | tf_op jit(solution)/shard_map/convert_element_type | solution.py:19
  34.0 2.4 convert_bitcast_fusion
  36.4 2.2 slice_bitcast_fusion.4
  38.5 6.4 %copy.74 = bf16[2,96,4,96,16]{3,4,2,1,0:T(8,128)(2,1)} copy(bf16[2,96,4,96,16]{1,4,3,2,0:T(8,128)(2,1)S(1)} %convert_bitcast_fusion) | data formatting | bytes 4718592 | tf_op jit(solution)/shard_map/while | solution.py:80
  44.9 4.3 %copy.70 = bf16[96,4,96,16]{2,3,1,0:T(8,128)(2,1)S(1)} copy(bf16[96,4,96,16]{0,3,2,1:T(8,128)(2,1)} %get-tuple-element.288) | data formatting | bytes 2359296 | tf_op jit(solution)/shard_map/squeeze | solution.py:36
  49.3 4.0 %copy.79 = bf16[96,96,64,1]{1,2,3,0:T(8,128)(2,1)} copy(bf16[96,96,64,1]{0,2,1,3:T(8,128)(2,1)S(1)} %copy-done.2) | data formatting | bytes 2359296 | tf_op jit(solution)/shard_map/convert_element_type | solution.py:19
  53.4 2.0 fusion.25
  55.4 4.0 %copy.69 = bf16[96,4,96,16]{2,3,1,0:T(8,128)(2,1)} copy(bf16[96,4,96,16]{0,3,1,2:T(8,128)(2,1)S(1)} %fusion.25) | data formatting | bytes 2359296 | tf_op jit(solution)/shard_map/convert_element_type | solution.py:20
  59.4 4.4 %copy.73 = bf16[96,4,96,16]{2,3,1,0:T(8,128)(2,1)S(1)} copy(bf16[96,4,96,16]{0,3,2,1:T(8,128)(2,1)} %get-tuple-element.287) | data formatting | bytes 2359296 | tf_op jit(solution)/shard_map/squeeze | solution.py:41
  65.8 2.0 copy.71
  68.7 10.4 %fusion.8 = (f32[96,4,96]{2,1,0:T(4,128)}, f32[96,4,96,96]{2,3,1,0:T(8,128)}) fusion(f32[96]{0:T(128)S(1)} %dynamic_slice.27, f32[4,96,96]{1,2,0:T(8,128)S(1)} %convert_bitcast_fusion.1, bf16[96,4,96,16]{2,3,1,0:T(8,128)(2,1)} %copy.69, bf16[96,4,96,16]{2,3,1,0:T(8,128)(2,1)S(1)} %copy.70), kind=kOutput, calls=%fused_computation.15 | convolution fusion | flops 123826176 | bytes 16810368 | tf_op jit(solution)/shard_map/jhid,jhkd->jhik/dot_general | solution.py:36
  79.1 12.5 %fusion.10 = f32[96,4,96]{2,1,0:T(4,128)S(1)} fusion(f32[96,4,96,96]{2,3,1,0:T(8,128)} %get-tuple-element.292, f32[96,4,96]{2,1,0:T(4,128)} %get-tuple-element.361, f32[96]{0:T(128)S(1)} %dynamic_slice.27, f32[4,96,96]{1,2,0:T(8,128)S(1)} %convert_bitcast_fusion.1), kind=kLoop, calls=%fused_computation.17 | loop fusion | flops 14118912 | bytes 14598528 | tf_op jit(solution)/shard_map/reduce_sum | solution.py:40
  91.6 1.7 exponential_multiply_fusion
  93.3 9.5 %fusion.21 = f32[96,4,96,16]{2,3,1,0:T(8,128)} fusion(bf16[96,4,96,16]{2,3,1,0:T(8,128)(2,1)S(1)} %copy.73, f32[96,4,96,96]{2,3,1,0:T(8,128)} %get-tuple-element.292, f32[96,4,96]{2,1,0:T(4,128)} %get-tuple-element.361, f32[96]{0:T(128)S(1)} %dynamic_slice.27, f32[4,96,96]{1,2,0:T(8,128)S(1)} %convert_bitcast_fusion.1, f32[96,4,96]{2,1,0:T(4,128)S(1)} %get-tuple-element.289), kind=kOutput, calls=%fused_computation.33 | convolution fusion | flops 127991808 | bytes 18137472 | tf_op jit(solution)/shard_map/jhik,jhkd->jhid/dot_general | solution.py:41
  102.8 229.8 %while.21 = (s32[]{:T(128)}, f32[96,4,96]{2,1,0:T(4,128)}, f32[96,4,96]{2,1,0:T(4,128)}, f32[96,4,96,16]{2,3,1,0:T(8,128)}, bf16[2,96,4,96,16]{3,4,2,1,0:T(8,128...) while((s32[]{:T(128)}, f32[96,4,96]{2,1,0:T(4,128)}, ...), condition=%wide.region_7.8_spmd, body=%wide.region_4.7_spmd.sunk | while | flops 266711056 | bytes 88553048 | solution.py:80
  105.4 34.6 %collective-permute-done = bf16[2,96,4,96,16]{3,4,2,1,0:T(8,128)(2,1)S(1)} collective-permute-done((bf16[2,96,4,96,16]{3,4,2,1,0:T(8,128)(2,1)}, bf16[2,96,4,96,16]{3,4,2,1,0:T(8,128)(2,1)S(1)}, u32[]{:S(2)}, u32[]{:S(2)}) %collective-permute-start) | collective-permute-done | bytes 2359328 | tf_op jit(solution)/shard_map/while/body/eval_jaxpr/ppermute | solution.py:77
  140.0 9.7 %fusion.55 = (f32[96,4,96]{2,1,0:T(4,128)S(1)}, f32[96,4,96,96]{2,3,1,0:T(8,128)}) fusion(f32[96]{0:T(128)S(1)} %dynamic_slice.33, f32[4,96,96]{1,2,0:T(8,128)S(1)} %dynamic-slice_convert_fusion.2, bf16[96,4,96,16]{2,3,1,0:T(8,128)(2,1)} %get-tuple-element.395, bf16[2,96,4,96,16]{3,4,2,1,0:T(8,128)(2,1)S(1)} %collective-permute-done), kind=kOutput, calls=%fused_computation.2.clone.1 | convolution fusion | flops 123826176 | bytes 17252864 | tf_op jit(solution)/shard_map/while/body/eval_jaxpr/jhid,jhkd->jhik/dot_general | solution.py:36
  149.7 1.0 max.11
  150.7 13.3 %fusion.56 = f32[96,4,96]{2,1,0:T(4,128)} fusion(f32[96,4,96,96]{2,3,1,0:T(8,128)} %get-tuple-element.357, f32[96,4,96]{2,1,0:T(4,128)S(1)} %max.11, f32[96]{0:T(128)} %copy-done.5, f32[4,96,96]{1,2,0:T(8,128)S(1)} %dynamic-slice_convert_fusion.2), kind=kLoop, calls=%fused_computation.4.clone.1 | loop fusion | flops 14118912 | bytes 14598528 | tf_op jit(solution)/shard_map/while/body/eval_jaxpr/reduce_sum | solution.py:40
  164.0 1.8 multiply_add_fusion.4
  166.6 1.7 copy.102
  168.2 1.4 copy-done.15
  169.6 8.4 %multiply_add_fusion.5 = f32[96,4,96,16]{2,3,1,0:T(8,128)S(1)} fusion(f32[96,4,96,16]{2,3,1,0:T(8,128)S(1)} %copy-done.15, f32[96,4,96,96]{2,3,1,0:T(8,128)} %get-tuple-element.357, f32[96,4,96]{2,1,0:T(4,128)S(1)} %max.11, f32[96]{0:T(128)S(1)} %copy-done.6, f32[4,96,96]{1,2,0:T(8,128)S(1)} %dynamic-slice_convert_fusion.2, ...), kind=kOutput, calls=%fused_computation.6.clone.1 | convolution fusion | flops 128581632 | bytes 21824000 | tf_op jit(solution)/shard_map/while/body/eval_jaxpr/jhik,jhkd->jhid/dot_general | solution.py:41
  178.0 1.7 copy-done.16
  181.3 35.1 %collective-permute-done = bf16[2,96,4,96,16]{3,4,2,1,0:T(8,128)(2,1)S(1)} collective-permute-done((bf16[2,96,4,96,16]{3,4,2,1,0:T(8,128)(2,1)}, bf16[2,96,4,96,16]{3,4,2,1,0:T(8,128)(2,1)S(1)}, u32[]{:S(2)}, u32[]{:S(2)}) %collective-permute-start) | collective-permute-done | bytes 2359328 | tf_op jit(solution)/shard_map/while/body/eval_jaxpr/ppermute | solution.py:77
  216.4 9.7 %fusion.55 = (f32[96,4,96]{2,1,0:T(4,128)S(1)}, f32[96,4,96,96]{2,3,1,0:T(8,128)}) fusion(f32[96]{0:T(128)S(1)} %dynamic_slice.33, f32[4,96,96]{1,2,0:T(8,128)S(1)} %dynamic-slice_convert_fusion.2, bf16[96,4,96,16]{2,3,1,0:T(8,128)(2,1)} %get-tuple-element.395, bf16[2,96,4,96,16]{3,4,2,1,0:T(8,128)(2,1)S(1)} %collective-permute-done), kind=kOutput, calls=%fused_computation.2.clone.1 | convolution fusion | flops 123826176 | bytes 17252864 | tf_op jit(solution)/shard_map/while/body/eval_jaxpr/jhid,jhkd->jhik/dot_general | solution.py:36
  226.1 1.0 max.11
  227.1 13.3 %fusion.56 = f32[96,4,96]{2,1,0:T(4,128)} fusion(f32[96,4,96,96]{2,3,1,0:T(8,128)} %get-tuple-element.357, f32[96,4,96]{2,1,0:T(4,128)S(1)} %max.11, f32[96]{0:T(128)} %copy-done.5, f32[4,96,96]{1,2,0:T(8,128)S(1)} %dynamic-slice_convert_fusion.2), kind=kLoop, calls=%fused_computation.4.clone.1 | loop fusion | flops 14118912 | bytes 14598528 | tf_op jit(solution)/shard_map/while/body/eval_jaxpr/reduce_sum | solution.py:40
  240.4 1.8 multiply_add_fusion.4
  243.0 1.7 copy.102
  244.6 1.4 copy-done.15
  246.0 8.4 %multiply_add_fusion.5 = f32[96,4,96,16]{2,3,1,0:T(8,128)S(1)} fusion(f32[96,4,96,16]{2,3,1,0:T(8,128)S(1)} %copy-done.15, f32[96,4,96,96]{2,3,1,0:T(8,128)} %get-tuple-element.357, f32[96,4,96]{2,1,0:T(4,128)S(1)} %max.11, f32[96]{0:T(128)S(1)} %copy-done.6, f32[4,96,96]{1,2,0:T(8,128)S(1)} %dynamic-slice_convert_fusion.2, ...), kind=kOutput, calls=%fused_computation.6.clone.1 | convolution fusion | flops 128581632 | bytes 21824000 | tf_op jit(solution)/shard_map/while/body/eval_jaxpr/jhik,jhkd->jhid/dot_general | solution.py:41
  254.4 1.7 copy-done.16
  257.7 35.1 %collective-permute-done = bf16[2,96,4,96,16]{3,4,2,1,0:T(8,128)(2,1)S(1)} collective-permute-done((bf16[2,96,4,96,16]{3,4,2,1,0:T(8,128)(2,1)}, bf16[2,96,4,96,16]{3,4,2,1,0:T(8,128)(2,1)S(1)}, u32[]{:S(2)}, u32[]{:S(2)}) %collective-permute-start) | collective-permute-done | bytes 2359328 | tf_op jit(solution)/shard_map/while/body/eval_jaxpr/ppermute | solution.py:77
  292.8 9.7 %fusion.55 = (f32[96,4,96]{2,1,0:T(4,128)S(1)}, f32[96,4,96,96]{2,3,1,0:T(8,128)}) fusion(f32[96]{0:T(128)S(1)} %dynamic_slice.33, f32[4,96,96]{1,2,0:T(8,128)S(1)} %dynamic-slice_convert_fusion.2, bf16[96,4,96,16]{2,3,1,0:T(8,128)(2,1)} %get-tuple-element.395, bf16[2,96,4,96,16]{3,4,2,1,0:T(8,128)(2,1)S(1)} %collective-permute-done), kind=kOutput, calls=%fused_computation.2.clone.1 | convolution fusion | flops 123826176 | bytes 17252864 | tf_op jit(solution)/shard_map/while/body/eval_jaxpr/jhid,jhkd->jhik/dot_general | solution.py:36
  302.5 1.0 max.11
  303.5 13.3 %fusion.56 = f32[96,4,96]{2,1,0:T(4,128)} fusion(f32[96,4,96,96]{2,3,1,0:T(8,128)} %get-tuple-element.357, f32[96,4,96]{2,1,0:T(4,128)S(1)} %max.11, f32[96]{0:T(128)} %copy-done.5, f32[4,96,96]{1,2,0:T(8,128)S(1)} %dynamic-slice_convert_fusion.2), kind=kLoop, calls=%fused_computation.4.clone.1 | loop fusion | flops 14118912 | bytes 14598528 | tf_op jit(solution)/shard_map/while/body/eval_jaxpr/reduce_sum | solution.py:40
  316.8 1.8 multiply_add_fusion.4
  319.3 1.7 copy.102
  321.0 1.4 copy-done.15
  322.4 8.4 %multiply_add_fusion.5 = f32[96,4,96,16]{2,3,1,0:T(8,128)S(1)} fusion(f32[96,4,96,16]{2,3,1,0:T(8,128)S(1)} %copy-done.15, f32[96,4,96,96]{2,3,1,0:T(8,128)} %get-tuple-element.357, f32[96,4,96]{2,1,0:T(4,128)S(1)} %max.11, f32[96]{0:T(128)S(1)} %copy-done.6, f32[4,96,96]{1,2,0:T(8,128)S(1)} %dynamic-slice_convert_fusion.2, ...), kind=kOutput, calls=%fused_computation.6.clone.1 | convolution fusion | flops 128581632 | bytes 21824000 | tf_op jit(solution)/shard_map/while/body/eval_jaxpr/jhik,jhkd->jhid/dot_general | solution.py:41
  330.8 1.7 copy-done.16
  332.6 5.2 %fusion.19 = bf16[96,96,64]{0,2,1:T(8,128)(2,1)S(1)} fusion(bf16[96,96,64]{0,2,1:T(8,128)(2,1)} %copy-done.1, bf16[4,16,64,1]{2,1,0,3:T(8,128)(2,1)S(1)} %bitcast.99, f32[96,4,96,16]{2,3,1,0:T(8,128)} %get-tuple-element.227, bf16[64,4,16,1]{0,2,1,3:T(8,128)(2,1)} %bitcast.108, f32[96,4,96]{2,1,0:T(4,128)} %get-tuple-element.228, f32[64]{0:T(128)} %param.15, ...), kind=kOutput, calls=%fused_computation.28 | convolution fusion | flops 159842304 | bytes 4956672 | tf_op jit(solution)/shard_map/jhid,hdc->ijc/dot_general | solution.py:50
  337.8 4.0 %copy.76 = bf16[96,96,64]{1,2,0:T(8,128)(2,1)} copy(bf16[96,96,64]{0,2,1:T(8,128)(2,1)S(1)} %fusion.19) | data formatting | bytes 2359296 | tf_op jit(solution)/shard_map/convert_element_type | solution.py:51
  (70 shorter events, 13.3 us)
Async XLA Ops:
  0.0 332.6 %copy-start = (bf16[64,64]{1,0:T(8,128)(2,1)S(1)}, bf16[64,64]{1,0:T(8,128)(2,1)}, u32[]{:S(2)}) copy-start(bf16[64,64]{1,0:T(8,128)(2,1)} %param.21) | copy-start | bytes 24580
  0.0 5.9 %copy-start.12 = (f32[64]{0:T(128)S(1)}, f32[64]{0:T(128)}, u32[]{:S(2)}) copy-start(f32[64]{0:T(128)} %param.14) | copy-start | bytes 772
  0.0 5.9 %copy-start.11 = (f32[64]{0:T(128)S(1)}, f32[64]{0:T(128)}, u32[]{:S(2)}) copy-start(f32[64]{0:T(128)} %param.15) | copy-start | bytes 772
  0.0 5.9 %copy-start.14 = (bf16[64,4]{0,1:T(4,128)(2,1)S(1)}, bf16[64,4]{0,1:T(4,128)(2,1)}, u32[]{:S(2)}) copy-start(bf16[64,4]{0,1:T(4,128)(2,1)} %param.19) | copy-start | bytes 1540
  4.5 23.4 %copy-start.1 = (bf16[96,96,64]{0,2,1:T(8,128)(2,1)}, bf16[96,96,64]{0,2,1:T(8,128)(2,1)S(1)}, u32[]{:S(2)}) copy-start(bf16[96,96,64]{0,2,1:T(8,128)(2,1)S(1)} %copy.62) | copy-start | bytes 3538948
  5.1 22.8 %copy-start.3 = (f32[96,96]{0,1:T(8,128)}, f32[96,96]{0,1:T(8,128)S(1)}, u32[]{:S(2)}) copy-start(f32[96,96]{0,1:T(8,128)S(1)} %broadcast_multiply_fusion) | copy-start | bytes 110596
  5.9 22.0 %copy-start.4 = (f32[96,96]{0,1:T(8,128)}, f32[96,96]{0,1:T(8,128)S(1)}, u32[]{:S(2)}) copy-start(f32[96,96]{0,1:T(8,128)S(1)} %add_rsqrt_fusion) | copy-start | bytes 110596
  22.9 42.9 %all-to-all-start = ((bf16[96,384,4]{0,2,1:T(4,128)(2,1)}), bf16[96,384,4]{0,2,1:T(4,128)(2,1)}, u32[]{:S(2)}, u32[]{:S(2)}) async-start(bf16[96,384,4]{0,2,1:T(4,128)(2,1)} %all_gather.3), calls=%async_computation | async-start | bytes 786432 | tf_op jit(solution)/shard_map/all_to_all | solution.py:30
  27.9 5.9 %copy-start.7 = (bf16[64,64]{1,0:T(8,128)(2,1)S(1)}, bf16[64,64]{1,0:T(8,128)(2,1)}, u32[]{:S(2)}) copy-start(bf16[64,64]{1,0:T(8,128)(2,1)} %param.17) | copy-start | bytes 24580
  27.9 6.0 %copy-start.8 = (bf16[64,64]{1,0:T(8,128)(2,1)S(1)}, bf16[64,64]{1,0:T(8,128)(2,1)}, u32[]{:S(2)}) copy-start(bf16[64,64]{1,0:T(8,128)(2,1)} %param.18) | copy-start | bytes 24580
  44.9 4.3 %copy-start.2 = (bf16[96,96,64,1]{0,2,1,3:T(8,128)(2,1)S(1)}, bf16[96,96,64,1]{0,2,1,3:T(8,128)(2,1)}, u32[]{:S(2)}) copy-start(bf16[96,96,64,1]{0,2,1,3:T(8,128)(2,1)} %fusion.45) | copy-start | bytes 3538948
  44.9 8.4 %copy-start.9 = (bf16[64,64]{1,0:T(8,128)(2,1)S(1)}, bf16[64,64]{1,0:T(8,128)(2,1)}, u32[]{:S(2)}) copy-start(bf16[64,64]{1,0:T(8,128)(2,1)} %param.16) | copy-start | bytes 24580
  55.4 8.5 %copy-start.10 = (bf16[64,64]{1,0:T(8,128)(2,1)S(1)}, bf16[64,64]{1,0:T(8,128)(2,1)}, u32[]{:S(2)}) copy-start(bf16[64,64]{1,0:T(8,128)(2,1)} %param.20) | copy-start | bytes 24580
  55.4 9.2 %copy-start.13 = (s32[384]{0:T(512)S(1)}, s32[384]{0:T(512)}, u32[]{:S(2)}) copy-start(s32[384]{0:T(512)} %param.13) | copy-start | bytes 4612
  103.2 36.7 %collective-permute-start = (bf16[2,96,4,96,16]{3,4,2,1,0:T(8,128)(2,1)}, bf16[2,96,4,96,16]{3,4,2,1,0:T(8,128)(2,1)S(1)}, u32[]{:S(2)}, u32[]{:S(2)}) collective-permute-start(bf16[2,96,4,96,16]{3,4,2,1,0:T(8,128)(2,1)} %get-tuple-element.379), channel_id=1, source_target_pairs={{0,1},{1,2},{2,3},{3,0},{4,5},{5,6},{6,7},{7,4},{8,9},{9,10},{10,1... | collective-permute-start | bytes 7077896 | tf_op jit(solution)/shard_map/while/body/eval_jaxpr/ppermute | solution.py:77
  104.5 45.3 %copy-start.5 = (f32[96]{0:T(128)}, f32[96]{0:T(128)S(1)}, u32[]{:S(2)}) copy-start(f32[96]{0:T(128)S(1)} %dynamic_slice.33) | copy-start | bytes 1156 | tf_op jit(solution)/shard_map/while
  166.6 1.7 copy-start.6
  166.6 3.0 copy-start.15
  178.0 1.7 copy-start.16
  179.7 36.7 %collective-permute-start = (bf16[2,96,4,96,16]{3,4,2,1,0:T(8,128)(2,1)}, bf16[2,96,4,96,16]{3,4,2,1,0:T(8,128)(2,1)S(1)}, u32[]{:S(2)}, u32[]{:S(2)}) collective-permute-start(bf16[2,96,4,96,16]{3,4,2,1,0:T(8,128)(2,1)} %get-tuple-element.379), channel_id=1, source_target_pairs={{0,1},{1,2},{2,3},{3,0},{4,5},{5,6},{6,7},{7,4},{8,9},{9,10},{10,1... | collective-permute-start | bytes 7077896 | tf_op jit(solution)/shard_map/while/body/eval_jaxpr/ppermute | solution.py:77
  180.4 45.7 %copy-start.5 = (f32[96]{0:T(128)}, f32[96]{0:T(128)S(1)}, u32[]{:S(2)}) copy-start(f32[96]{0:T(128)S(1)} %dynamic_slice.33) | copy-start | bytes 1156 | tf_op jit(solution)/shard_map/while
  243.0 1.7 copy-start.6
  243.0 3.0 copy-start.15
  254.4 1.7 copy-start.16
  256.1 36.7 %collective-permute-start = (bf16[2,96,4,96,16]{3,4,2,1,0:T(8,128)(2,1)}, bf16[2,96,4,96,16]{3,4,2,1,0:T(8,128)(2,1)S(1)}, u32[]{:S(2)}, u32[]{:S(2)}) collective-permute-start(bf16[2,96,4,96,16]{3,4,2,1,0:T(8,128)(2,1)} %get-tuple-element.379), channel_id=1, source_target_pairs={{0,1},{1,2},{2,3},{3,0},{4,5},{5,6},{6,7},{7,4},{8,9},{9,10},{10,1... | collective-permute-start | bytes 7077896 | tf_op jit(solution)/shard_map/while/body/eval_jaxpr/ppermute | solution.py:77
  256.8 45.7 %copy-start.5 = (f32[96]{0:T(128)}, f32[96]{0:T(128)S(1)}, u32[]{:S(2)}) copy-start(f32[96]{0:T(128)S(1)} %dynamic_slice.33) | copy-start | bytes 1156 | tf_op jit(solution)/shard_map/while
  319.3 1.7 copy-start.6
  319.3 3.0 copy-start.15
  330.8 1.7 copy-start.16
where the time goes:
time: 346 us; the launch traced here: 342 us
  waiting for transfers between devices  105 us (30%)
  matrix products  84.5 us (24%)
  other arithmetic  70.6 us (20%)
  local copies, waits for them, and re-layouts  59.8 us (17%)
  blocking collectives  16.3 us (5%)
  starting transfers between devices  4.81 us (1%)
    ppermute x3, waiting for transfers between devices, shift_step(): kv_blk = lax.ppermute(kv_blk, 'row', next_hop)  105 us
    reduce_sum x4, other arithmetic, attend_block(): run_sum = run_sum * rescale + jnp.sum(p_exp, axis=-1)  52.4 us
    dot_general x4, matrix products, attend_block(): jnp.einsum('jhid,jhkd->jhik', query, kv_blk[0], preferred_element_type=jn...  39.6 us
    dot_general x4, matrix products, attend_block(): jnp.einsum('jhik,jhkd->jhid', p_exp.astype(jnp.bfloat16), kv_blk[1], pref...  34.7 us
    all_gather x1, blocking collectives, bias_strip(): full_cols = lax.all_gather(bias_tile, 'col', axis=1, tiled=True)  16.3 us
    while x30, local copies, waits for them, and re-layouts  16.2 us
    convert_element_type x2, local copies, waits for them, and re-layouts, norm_and_project(): (centred * lax.rsqrt(variance + LN_EPS) * ln_gamma + ln_beta).astype(jnp....  8.08 us
  transfers between devices with their start and end apart: 4, of which 3 were waited for; matrix products, arithmetic and copies ran while one was open for 13% of the time, Pallas kernels for 0%

commit v1 on v0

v1 whole, which is shorter than its diff:
```python
import functools
import math

import jax
import jax.numpy as jnp
from jax import lax
from jax.experimental import pallas as pl
from jax.experimental.pallas import tpu as pltpu
from jax.sharding import PartitionSpec as P

LN_EPS = 1e-5
MASK_FILL = -1e9
LOG2E = math.log2(math.e)
HEADS = 4
HD = 16
C = 64
NB = 96
NK = 384
NQ = 192
PAIRS = 24
CHUNK = 4
NCH = PAIRS // CHUNK
MESH = pl.DeviceIdType.MESH
F32 = jnp.float32
BF16 = jnp.bfloat16


def dot(a, b, ca=1, cb=0):
    return lax.dot_general(a, b, (((ca,), (cb,)), ((), ())), preferred_element_type=F32)


def kernel(a_ref, bt_ref, fill_ref, wkt_ref, wv_ref, wqg_ref, g_ref,
           a_all, bias_in, bias_f, kbd, vbd, p_ref, g_send, g_recv,
           a_ssem, a_rsem, b_ssem, b_rsem, f_ssem, g_ssem, g_rsem):
    col = lax.axis_index("col")
    row = lax.axis_index("row")
    y, s = row // 2, lax.rem(row, 2)
    u_own = lax.rem(col, 2)
    y_tgt = col // 2
    partner = y * 2 + (1 - s)
    across = (1 - y) * 2 + s
    cross = (1 - y) * 2 + (1 - s)
    peers = (partner, across, cross)

    barrier = pltpu.get_barrier_semaphore()
    for r in peers:
        pl.semaphore_signal(barrier, inc=1, device_id={"row": r}, device_id_type=MESH)
    for d in range(1, 4):
        pl.semaphore_signal(barrier, inc=1, device_id={"col": lax.rem(col + d, 4)}, device_id_type=MESH)

    a_all[:, pl.ds(pl.multiple_of(row * NB, NB), NB), :] = a_ref[pl.ds(s * PAIRS, PAIRS)]
    kbd[...] = jnp.zeros_like(kbd)
    pl.semaphore_wait(barrier, 6)

    def bias_copy(src, u, r, ssem, dev):
        return pltpu.make_async_remote_copy(
            src_ref=src, dst_ref=bias_in.at[u, r], send_sem=ssem, recv_sem=b_rsem.at[u, r],
            device_id=dev, device_id_type=MESH)

    def bias_wait(u, r):
        bias_copy(bias_in.at[u, r], u, r, b_ssem.at[0], {"row": partner}).wait_recv()

    is_src = y_tgt == y

    @pl.when(jnp.logical_not(is_src))
    def _():
        bias_copy(bt_ref, u_own, row, b_ssem.at[0], {"row": across}).start()

    def a_copy(slot, q, r):
        s_d = lax.rem(r, 2)
        return pltpu.make_async_remote_copy(
            src_ref=a_ref.at[pl.ds(s_d * PAIRS + q * CHUNK, CHUNK)],
            dst_ref=a_all.at[pl.ds(q * CHUNK, CHUNK), pl.ds(pl.multiple_of(row * NB, NB), NB)],
            send_sem=a_ssem.at[slot, q], recv_sem=a_rsem.at[slot, q],
            device_id={"row": r}, device_id_type=MESH)

    def a_wait_recv(slot, q, r):
        pltpu.make_async_remote_copy(
            src_ref=a_ref.at[pl.ds(0, CHUNK)],
            dst_ref=a_all.at[pl.ds(q * CHUNK, CHUNK), pl.ds(pl.multiple_of(r * NB, NB), NB)],
            send_sem=a_ssem.at[slot, q], recv_sem=a_rsem.at[slot, q],
            device_id={"row": r}, device_id_type=MESH).wait_recv()

    for q in range(NCH):
        for slot, r in enumerate(peers):
            a_copy(slot, q, r).start()

    @pl.when(is_src)
    def _():
        bias_in[u_own, row] = bt_ref[...]
        for d in range(1, 4):
            bias_copy(bt_ref, u_own, row, b_ssem.at[d], {"col": lax.rem(col + d, 4)}).start()
        bias_wait(u_own, across)
        for d in range(1, 4):
            bias_copy(bias_in.at[u_own, across], u_own, across, b_ssem.at[3 + d],
                      {"col": lax.rem(col + d, 4)}).start()
        bias_wait(1 - u_own, row)
        bias_wait(1 - u_own, across)

    @pl.when(jnp.logical_not(is_src))
    def _():
        for u in range(2):
            bias_wait(u, row)
            bias_wait(u, across)

    for u in range(2):
        for i, r in enumerate((row, across)):
            bias_copy(bias_in.at[u, r], u, r, f_ssem.at[u, i], {"row": partner}).start()
    for u in range(2):
        for r in (partner, cross):
            bias_wait(u, r)

    lane = lax.broadcasted_iota(jnp.int32, (NB, 128), 1)
    for u in range(2):
        for h in range(HEADS):
            t = [bias_in[u, r, :, h * 128:(h + 1) * 128].astype(F32) for r in range(4)]
            parts = (jnp.where(lane < 96, t[0], t[1]), jnp.where(lane < 64, t[1], t[2]),
                     jnp.where(lane < 32, t[2], t[3]))
            for i, part in enumerate(parts):
                sl = slice(i * 128, (i + 1) * 128)
                bias_f[h, u * NB:(u + 1) * NB, sl] = (part + fill_ref[:, sl]) * LOG2E

    hid = lax.broadcasted_iota(jnp.int32, (NK, C), 1) // HD
    hid_q = lax.broadcasted_iota(jnp.int32, (NQ, C), 1) // HD

    def pair(p):
        x = a_all[p]
        xq = a_all[p, pl.ds(pl.multiple_of(y * NQ, NQ), NQ), :]
        qg = dot(xq, wqg_ref[...])
        q2 = (qg[:, :128] * (1.0 / math.sqrt(HD))).astype(BF16)
        v2 = dot(x, wv_ref[...]).astype(BF16)
        kt = dot(wkt_ref[...], x, 1, 1).astype(BF16)
        gated = []
        for jj in range(2):
            q_j = q2[:, jj * C:(jj + 1) * C]
            v_j = v2[:, jj * C:(jj + 1) * C]
            for h in range(HEADS):
                kbd[h * HD:(h + 1) * HD, h * NK:(h + 1) * NK] = kt[jj * C + h * HD:jj * C + (h + 1) * HD, :]
                vbd[h * NK:(h + 1) * NK, :] = jnp.where(hid == h, v_j, jnp.zeros_like(v_j))
            inv = []
            for hp in range(2):
                logits = dot(q_j, kbd[:, hp * 2 * NK:(hp + 1) * 2 * NK])
                for hh in range(2):
                    h = hp * 2 + hh
                    t = logits[:, hh * NK:(hh + 1) * NK] * LOG2E + bias_f[h]
                    m = jnp.max(t, axis=1, keepdims=True)
                    e = jnp.exp2(t - m)
                    inv.append(1.0 / jnp.sum(e, axis=1, keepdims=True))
                    p_ref[:, h * NK:(h + 1) * NK] = e.astype(BF16)
            o = dot(p_ref[...], vbd[...])
            scale = jnp.where(hid_q == 0, inv[0], jnp.where(hid_q == 1, inv[1], jnp.where(hid_q == 2, inv[2], inv[3])))
            gate = jax.nn.sigmoid(qg[:, 128 + jj * C:128 + (jj + 1) * C])
            gated.append(gate * (o * scale))
        return jnp.concatenate(gated, axis=1).astype(BF16)

    def g_copy(q):
        return pltpu.make_async_remote_copy(
            src_ref=g_send.at[pl.ds(q * CHUNK, CHUNK)], dst_ref=g_recv.at[pl.ds(q * CHUNK, CHUNK)],
            send_sem=g_ssem.at[q], recv_sem=g_rsem.at[q], device_id={"row": partner}, device_id_type=MESH)

    @pl.loop(0, NCH)
    def _(q):
        for slot, r in enumerate(peers):
            a_wait_recv(slot, q, r)

        @pl.loop(0, CHUNK)
        def _(i):
            p = q * CHUNK + i
            res = pair(p)
            g_ref[s * PAIRS + p] = jnp.where(s == 0, res[:NB], res[NB:])
            g_send[p] = jnp.where(s == 0, res[NB:], res[:NB])

        g_copy(q).start()

    for q in range(NCH):
        g_copy(q).wait_recv()
    g_ref[pl.ds((1 - s) * PAIRS, PAIRS)] = g_recv[...]
    for q in range(NCH):
        g_copy(q).wait_send()
        for slot, r in enumerate(peers):
            a_copy(slot, q, r).wait_send()

    @pl.when(is_src)
    def _():
        for d in range(1, 7):
            bias_copy(bt_ref, u_own, row, b_ssem.at[d], {"row": partner}).wait_send()

    @pl.when(jnp.logical_not(is_src))
    def _():
        bias_copy(bt_ref, u_own, row, b_ssem.at[0], {"row": across}).wait_send()

    for u in range(2):
        for i, r in enumerate((row, across)):
            bias_copy(bias_in.at[u, r], u, r, f_ssem.at[u, i], {"row": partner}).wait_send()


def attend(a2, bt, fill, wkt, wv, wqg):
    vm = pl.BlockSpec(memory_space=pltpu.VMEM)
    dma = pltpu.SemaphoreType.DMA
    return pl.pallas_call(
        kernel,
        out_shape=jax.ShapeDtypeStruct((2 * PAIRS, NB, 128), BF16),
        in_specs=[vm] * 6,
        out_specs=vm,
        scratch_shapes=[
            pltpu.VMEM((PAIRS, NK, 128), BF16),
            pltpu.VMEM((2, 4, NB, HEADS * 128), BF16),
            pltpu.VMEM((HEADS, NQ, NK), F32),
            pltpu.VMEM((C, HEADS * NK), BF16),
            pltpu.VMEM((HEADS * NK, C), BF16),
            pltpu.VMEM((NQ, HEADS * NK), BF16),
            pltpu.VMEM((PAIRS, NB, 128), BF16),
            pltpu.VMEM((PAIRS, NB, 128), BF16),
            dma((3, NCH)), dma((3, NCH)), dma((7,)), dma((2, 4)), dma((2, 2)), dma((NCH,)), dma((NCH,)),
        ],
        compiler_params=pltpu.CompilerParams(collective_id=0, has_side_effects=True, vmem_limit_bytes=56 * 2**20),
        name="attend",
    )(a2, bt, fill, wkt, wv, wqg)


def blockdiag2(w):
    z = jnp.zeros_like(w)
    return jnp.concatenate([jnp.concatenate([w, z], 1), jnp.concatenate([z, w], 1)], 0)


def solution(mesh):
    def body(pair_tile, res_mask, ln_gamma, ln_beta, w_q, w_k, w_v, w_b, w_g, w_o):
        row = lax.axis_index("row")
        pair_f32 = pair_tile.astype(F32)
        mean = jnp.mean(pair_f32, axis=-1, keepdims=True)
        centred = pair_f32 - mean
        variance = jnp.mean(centred * centred, axis=-1, keepdims=True)
        normed = (centred * lax.rsqrt(variance + LN_EPS) * ln_gamma + ln_beta).astype(BF16)
        a2 = jnp.transpose(normed.reshape(NB, NB // 2, 128), (1, 0, 2))
        bias = jnp.einsum("kic,ch->ihk", normed, w_b, preferred_element_type=F32).astype(BF16)
        bias = jnp.pad(bias, ((0, 0), (0, 0), (0, 128 - NB)))
        bias = jnp.roll(bias, lax.rem(row * NB, 128), axis=2).reshape(NB, HEADS * 128)
        fill = jnp.where(res_mask > 0, 0.0, MASK_FILL).astype(F32)[None, :]
        wqg = jnp.concatenate([blockdiag2(w_q), blockdiag2(w_g)], 1)
        gated = attend(a2, bias, fill, blockdiag2(w_k.T), blockdiag2(w_v), wqg)
        gated = jnp.transpose(gated, (1, 0, 2)).reshape(NB, NB, C)
        update = jnp.einsum("ijd,dc->ijc", gated, w_o, preferred_element_type=F32)
        return (pair_f32 + update).astype(BF16)

    tile_spec = P(("data", "row"), "col", None)
    return jax.shard_map(body, mesh=mesh, in_specs=(tile_spec, P("data"), P(), P(), P(), P(), P(), P(), P(), P()),
                         out_specs=tile_spec, check_vma=False)
```

time: 346 us -> 84.5 us (0.24)
  the two profiles are of different devices: /device:TPU:0 before, /device:TPU:27 now
where the time goes in v1:
time: 84.5 us; the launch traced here: 84.3 us
  Pallas kernels  60.9 us (72%)
  local copies, waits for them, and re-layouts  14 us (17%)
  other arithmetic  5.82 us (7%)
  matrix products  3.49 us (4%)
    pallas_call x1, Pallas kernels, attend(): pl.pallas_call(kernel, out_shape=jax.ShapeDtypeStruct((2 * PAIRS, NB, 128...  60.9 us
    reshape x1, local copies, waits for them, and re-layouts, body(): gated = jnp.transpose(gated, (1, 0, 2)).reshape(NB, NB, C)  4.04 us
    convert_element_type x1, local copies, waits for them, and re-layouts, body(): (centred * lax.rsqrt(variance + LN_EPS) * ln_gamma + ln_beta).astype(BF16)  3.98 us
    dot_general x1, matrix products, body(): update = jnp.einsum('ijd,dc->ijc', gated, w_o, preferred_element_type=F32)  3.17 us
    reshape x1, local copies, waits for them, and re-layouts, body(): a2 = jnp.transpose(normed.reshape(NB, NB // 2, 128), (1, 0, 2))  2.55 us
    reduce_sum x1, other arithmetic, body(): mean = jnp.mean(pair_f32, axis=-1, keepdims=True)  2.06 us
    transpose x1, local copies, waits for them, and re-layouts, body(): gated = jnp.transpose(gated, (1, 0, 2)).reshape(NB, NB, C)  1.85 us

profile of v1, /device:TPU:27, one launch (start us, length us, event | category | flops | bytes accessed | tf_op | source)
XLA Modules:
  0.0 84.3 jit_solution(8207524906822433873)
XLA Ops:
  0.0 0.0 copy-start
  0.0 0.0 copy-start.1
  0.0 0.0 copy-start.8
  0.0 0.0 copy-start.9
  0.0 2.1 %convert_reduce_fusion = f32[96,96]{1,0:T(8,128)S(1)} fusion(bf16[96,96,64]{1,2,0:T(8,128)(2,1)} %param.10), kind=kLoop, calls=%fused_computation.2 | loop fusion | flops 1170432 | bytes 1216512 | tf_op jit(solution)/shard_map/reduce_sum | solution.py:230
  2.1 0.0 copy-done.1
  2.1 0.8 fusion.2
  2.9 0.0 copy-done.8
  2.9 0.0 copy-done.9
  2.9 0.0 copy-start.7
  3.0 0.7 fusion.5
  3.7 0.0 copy-done.7
  3.7 0.3 fusion.7
  4.0 0.1 pad.12
  4.1 0.8 fusion.8
  4.9 0.1 copy.16
  5.0 0.6 copy.25
  5.7 4.0 %copy.14 = bf16[96,96,64]{0,2,1:T(8,128)(2,1)} copy(bf16[96,96,64]{1,2,0:T(8,128)(2,1)S(1)} %fusion.5) | data formatting | bytes 2359296 | tf_op jit(solution)/shard_map/convert_element_type | solution.py:233
  9.7 0.0 copy-start.2
  9.7 0.0 copy-start.3
  9.7 0.0 copy-start.4
  9.7 0.0 copy-start.5
  9.7 0.0 copy-start.6
  9.7 2.5 %copy.15 = bf16[96,48,128]{2,0,1:T(8,128)(2,1)} copy(bf16[96,48,128]{0,2,1:T(8,128)(2,1)} %bitcast.19) | data formatting | bytes 2359296 | tf_op jit(solution)/shard_map/reshape | solution.py:234
  12.2 0.0 copy-done.2
  12.2 0.1 copy.17
  12.3 0.0 copy-done.3
  12.3 0.7 fusion.28
  13.0 0.0 copy-done.4
  13.0 0.0 copy-done.5
  13.0 0.7 fusion.22.wqg_ref
  13.8 0.0 copy-done.6
  13.8 0.6 broadcast_in_dim.17.fill_ref
  14.3 60.9 %attend.1 = bf16[48,96,128]{2,1,0:T(8,128)(2,1)} custom-call(bf16[48,96,128]{2,1,0:T(8,128)(2,1)} %bitcast.21, bf16[96,512]{1,0:T(8,128)(2,1)} %bitcast.24, f32[1,384]{1,0:T(1,128)} %broadcast_in_dim.17.fill_ref, bf16[128,128]{1,0:T(8,128)(2,1)} %get-tuple-element.5.wkt_ref, bf16[128,128]{1,0:T(8,128)(2,1)} %get-tuple-element.6.wv_ref, ...), custom_call_target="tpu_custom_call" | custom-call | tf_op jit(solution)/shard_map/attend/pallas_call | solution.py:200
  75.2 1.9 %copy.18 = bf16[96,48,128]{0,2,1:T(8,128)(2,1)S(1)} copy(bf16[96,48,128]{2,0,1:T(8,128)(2,1)} %bitcast.22) | data formatting | bytes 2359296 | tf_op jit(solution)/shard_map/transpose | solution.py:241
  77.1 4.0 %copy.19 = bf16[96,96,64]{1,2,0:T(8,128)(2,1)} copy(bf16[96,96,64]{0,2,1:T(8,128)(2,1)S(1)} %bitcast.20) | data formatting | bytes 2359296 | tf_op jit(solution)/shard_map/reshape | solution.py:241
  81.1 0.0 copy-done
  81.2 3.2 %fusion.6 = bf16[96,96,64]{1,2,0:T(8,128)(2,1)} fusion(bf16[96,96,64]{1,2,0:T(8,128)(2,1)S(1)} %copy-done.1, bf16[96,96,64]{1,2,0:T(8,128)(2,1)} %copy.19, bf16[64,64]{1,0:T(8,128)(2,1)S(1)} %copy-done), kind=kOutput, calls=%fused_computation.9 | convolution fusion | flops 77266944 | bytes 3547136 | tf_op jit(solution)/shard_map/ijd,dc->ijc/dot_general | solution.py:242
  (3 shorter events, 0.0 us)
Async XLA Ops:
  0.0 81.2 %copy-start = (bf16[64,64]{1,0:T(8,128)(2,1)S(1)}, bf16[64,64]{1,0:T(8,128)(2,1)}, u32[]{:S(2)}) copy-start(bf16[64,64]{1,0:T(8,128)(2,1)} %param.19) | copy-start | bytes 24580
  0.0 2.1 %copy-start.1 = (bf16[96,96,64]{1,2,0:T(8,128)(2,1)S(1)}, bf16[96,96,64]{1,2,0:T(8,128)(2,1)}, u32[]{:S(2)}) copy-start(bf16[96,96,64]{1,2,0:T(8,128)(2,1)} %param.10) | copy-start | bytes 3538948
  0.0 2.9 %copy-start.8 = (f32[64]{0:T(128)S(1)}, f32[64]{0:T(128)}, u32[]{:S(2)}) copy-start(f32[64]{0:T(128)} %param.13) | copy-start | bytes 772
  0.0 2.9 %copy-start.9 = (f32[64]{0:T(128)S(1)}, f32[64]{0:T(128)}, u32[]{:S(2)}) copy-start(f32[64]{0:T(128)} %param.12) | copy-start | bytes 772
  2.9 0.8 copy-start.7
  9.7 2.6 %copy-start.2 = (bf16[64,64]{1,0:T(8,128)(2,1)S(1)}, bf16[64,64]{1,0:T(8,128)(2,1)}, u32[]{:S(2)}) copy-start(bf16[64,64]{1,0:T(8,128)(2,1)} %param.15) | copy-start | bytes 24580
  9.7 2.7 %copy-start.3 = (bf16[64,64]{1,0:T(8,128)(2,1)S(1)}, bf16[64,64]{1,0:T(8,128)(2,1)}, u32[]{:S(2)}) copy-start(bf16[64,64]{1,0:T(8,128)(2,1)} %param.16) | copy-start | bytes 24580
  9.7 3.4 %copy-start.4 = (bf16[64,64]{1,0:T(8,128)(2,1)S(1)}, bf16[64,64]{1,0:T(8,128)(2,1)}, u32[]{:S(2)}) copy-start(bf16[64,64]{1,0:T(8,128)(2,1)} %param.18) | copy-start | bytes 24580
  9.7 3.4 %copy-start.5 = (bf16[64,64]{1,0:T(8,128)(2,1)S(1)}, bf16[64,64]{1,0:T(8,128)(2,1)}, u32[]{:S(2)}) copy-start(bf16[64,64]{1,0:T(8,128)(2,1)} %param.14) | copy-start | bytes 24580
  9.7 4.1 %copy-start.6 = (s32[384]{0:T(512)S(1)}, s32[384]{0:T(512)}, u32[]{:S(2)}) copy-start(s32[384]{0:T(512)} %param.11) | copy-start | bytes 4612

commit v2 on v1

v2 whole, which is shorter than its diff:
```python
import math

import jax
import jax.numpy as jnp
from jax import lax
from jax.experimental import pallas as pl
from jax.experimental.pallas import tpu as pltpu
from jax.sharding import PartitionSpec as P

LN_EPS = 1e-5
MASK_FILL = -1e9
LOG2E = math.log2(math.e)
HEADS = 4
HD = 16
C = 64
NB = 96
NK = 384
PAIRS = 24
CHUNK = 4
NCH = PAIRS // CHUNK
L = 128
MESH = pl.DeviceIdType.MESH
F32 = jnp.float32
BF16 = jnp.bfloat16


def dot(a, b, ca=1, cb=0):
    return lax.dot_general(a, b, (((ca,), (cb,)), ((), ())), preferred_element_type=F32)


def blockdiag2(w):
    z = jnp.zeros_like(w)
    return jnp.concatenate([jnp.concatenate([w, z], 1), jnp.concatenate([z, w], 1)], 0)


def transposed(w):
    return jnp.transpose(w.astype(F32)).astype(BF16)


def down(v, n):
    return jnp.transpose(jnp.broadcast_to(v.reshape(1, n), (L, n)))


def kernel(z_ref, mask_ref, gam_ref, bet_ref, wq_ref, wk_ref, wv_ref, wbt_ref, wg_ref, wo_ref, out_ref,
           t_sc, b_sc, a_own, a_all, b_own, bias_in, bias_f, qbd, g_send, g_recv, gf, wk2, wv2, wqg2, wo2,
           a_ssem, a_rsem, b1_ssem, b_ssem, b_rsem, f_ssem, g_ssem, g_rsem):
    col = lax.axis_index("col")
    row = lax.axis_index("row")
    y, s = row // 2, lax.rem(row, 2)
    partner = y * 2 + (1 - s)
    across = (1 - y) * 2 + s
    cross = (1 - y) * 2 + (1 - s)
    peers = (partner, across, cross)

    barrier = pltpu.get_barrier_semaphore()
    for r in peers:
        pl.semaphore_signal(barrier, inc=1, device_id={"row": r}, device_id_type=MESH)

    @pl.when(col > 0)
    def _():
        pl.semaphore_signal(barrier, inc=1, device_id={"col": col - 1}, device_id_type=MESH)

    @pl.when(col < 3)
    def _():
        pl.semaphore_signal(barrier, inc=1, device_id={"col": col + 1}, device_id_type=MESH)

    gam = down(gam_ref[...], C)[:, :NB]
    bet = down(bet_ref[...], C)[:, :NB]
    wbt = wbt_ref[...]

    @pl.loop(0, NB, unroll=4)
    def _(i):
        z = z_ref[i].astype(F32)
        mean = jnp.sum(z, axis=0, keepdims=True) * (1.0 / C)
        cen = z - mean
        var = jnp.sum(cen * cen, axis=0, keepdims=True) * (1.0 / C)
        a = cen * lax.rsqrt(var + LN_EPS) * gam + bet
        b_sc[i, :HEADS, :NB] = dot(wbt, a.astype(BF16))
        at = jnp.transpose(a)
        for half in range(2):
            o = half * 48
            t_sc[pl.ds(pl.multiple_of(i * 48 + half * PAIRS, 8), PAIRS), :] = jnp.concatenate(
                [at[o:o + PAIRS], at[o + PAIRS:o + 2 * PAIRS]], axis=1)

    @pl.loop(0, 2 * PAIRS, unroll=4)
    def _(n):
        a_own[n] = t_sc[pl.ds(n, NB, stride=2 * PAIRS), :].astype(BF16)

    lane = lax.broadcasted_iota(jnp.int32, (NB, L), 1)
    bh = [b_sc.reshape(NB * 8, L)[pl.ds(h, NB, stride=8), :] for h in range(HEADS)]
    for g in range(3):
        b_own[g] = jnp.where(lane < NB, bh[g], pltpu.roll(bh[3], NB - 32 * g, 1)).astype(BF16)

    wk2[...] = blockdiag2(wk_ref[...])
    wv2[...] = blockdiag2(transposed(wv_ref[...]))
    wqg2[:L] = blockdiag2(transposed(wq_ref[...]))
    wqg2[L:] = blockdiag2(transposed(wg_ref[...]))
    wo2[...] = blockdiag2(transposed(wo_ref[...]))
    qbd[...] = jnp.zeros_like(qbd)
    gf[...] = jnp.zeros_like(gf)
    a_all[:, NK:, :] = jnp.zeros((PAIRS, 32, L), BF16)
    a_all[:, pl.ds(pl.multiple_of(row * NB, NB), NB), :] = a_own[pl.ds(s * PAIRS, PAIRS)]

    pl.semaphore_wait(barrier, 3 + jnp.where(col > 0, 1, 0) + jnp.where(col < 3, 1, 0))

    def bias_copy(src, u, r, ssem, dev):
        return pltpu.make_async_remote_copy(
            src_ref=src, dst_ref=bias_in.at[u, r], send_sem=ssem, recv_sem=b_rsem.at[u, r],
            device_id=dev, device_id_type=MESH)

    def bias_wait(u, r):
        bias_copy(bias_in.at[u, r], u, r, b1_ssem, {"row": partner}).wait_recv()

    y_tgt = col // 2
    u_own = lax.rem(col, 2)
    is_src = y_tgt == y

    @pl.when(jnp.logical_not(is_src))
    def _():
        bias_copy(b_own, u_own, row, b1_ssem, {"row": across}).start()

    def a_copy(slot, q, r):
        s_d = lax.rem(r, 2)
        return pltpu.make_async_remote_copy(
            src_ref=a_own.at[pl.ds(s_d * PAIRS + q * CHUNK, CHUNK)],
            dst_ref=a_all.at[pl.ds(q * CHUNK, CHUNK), pl.ds(pl.multiple_of(row * NB, NB), NB)],
            send_sem=a_ssem.at[slot, q], recv_sem=a_rsem.at[slot, q],
            device_id={"row": r}, device_id_type=MESH)

    def a_wait_recv(slot, q, r):
        pltpu.make_async_remote_copy(
            src_ref=a_own.at[pl.ds(0, CHUNK)],
            dst_ref=a_all.at[pl.ds(q * CHUNK, CHUNK), pl.ds(pl.multiple_of(r * NB, NB), NB)],
            send_sem=a_ssem.at[slot, q], recv_sem=a_rsem.at[slot, q],
            device_id={"row": r}, device_id_type=MESH).wait_recv()

    for q in range(NCH):
        for slot, r in enumerate(peers):
            a_copy(slot, q, r).start()

    mine = (row, across)

    def right(u, i):
        return bias_copy(bias_in.at[u, mine[i]], u, mine[i], b_ssem.at[u, i, 0], {"col": jnp.minimum(col + 1, 3)})

    def left(u, i):
        return bias_copy(bias_in.at[u, mine[i]], u, mine[i], b_ssem.at[u, i, 1], {"col": jnp.maximum(col - 1, 0)})

    def to_partner(u, i):
        return bias_copy(bias_in.at[u, mine[i]], u, mine[i], f_ssem.at[u, i], {"row": partner})

    def sends_right(u):
        return jnp.logical_and(col >= 2 * y + u, col < 3)

    def sends_left(u):
        return jnp.logical_and(col <= 2 * y + u, col > 0)

    @pl.when(is_src)
    def _():
        bias_in[u_own, row] = b_own[...]

    for i in range(2):
        for u in range(2):
            own = jnp.logical_and(is_src, u_own == u)
            if i == 0:
                @pl.when(jnp.logical_not(own))
                def _(u=u, i=i):
                    bias_wait(u, mine[i])
            else:
                bias_wait(u, mine[i])

            @pl.when(sends_right(u))
            def _(u=u, i=i):
                right(u, i).start()

            @pl.when(sends_left(u))
            def _(u=u, i=i):
                left(u, i).start()

            to_partner(u, i).start()

    for u in range(2):
        for r in (partner, cross):
            bias_wait(u, r)

    fill = down(jnp.where(mask_ref[...] > 0, 0.0, MASK_FILL).astype(F32), NK)
    for r in range(4):
        for u in range(2):
            for g in range(3):
                sl = slice(r * NB, (r + 1) * NB)
                bias_f[u, g, sl, :] = (bias_in[u, r, g].astype(F32) + fill[sl]) * LOG2E

    lane16 = lax.broadcasted_iota(jnp.int32, (HD, L), 1)

    def pair(p):
        x = a_all[p, :NK, :]
        k2 = dot(x, wk2[...]).astype(BF16)
        vt = dot(wv2[...], x, 1, 1).astype(BF16)
        gate = []
        for u in range(2):
            xu = a_all[p, pl.ds(pl.multiple_of((2 * y + u) * NB, NB), L), :]
            qg = dot(wqg2[...], xu, 1, 1)
            qt = qg[:L] * (1.0 / math.sqrt(HD))
            gate.append(jax.nn.sigmoid(qg[L:]))
            for t in range(2):
                q3 = qt[t * C + 48:t * C + 64]
                for g in range(3):
                    o = (g * 2 + u) * L
                    qgh = qt[t * C + g * HD:t * C + (g + 1) * HD]
                    qbd[t, t * C + g * HD:t * C + (g + 1) * HD, o:o + L] = jnp.where(lane16 < NB, qgh, 0.0).astype(BF16)
                    qbd[t, t * C + 48:t * C + 64, o:o + L] = jnp.where(
                        lane16 < NB, 0.0, pltpu.roll(q3, NB - 32 * g, 1)).astype(BF16)
        att = [[], []]
        for t in range(2):
            o_t = []
            for g in range(3):
                logits = dot(k2, qbd[t, :, g * 2 * L:(g + 1) * 2 * L])
                lt = logits * LOG2E + jnp.concatenate([bias_f[0, g], bias_f[1, g]], axis=1)
                m = jnp.max(lt, axis=0, keepdims=True)
                e = jnp.exp2(lt - m)
                inv = 1.0 / jnp.sum(e, axis=0, keepdims=True)
                vg = jnp.concatenate([vt[t * C + g * HD:t * C + (g + 1) * HD], vt[t * C + 48:t * C + 64]], axis=0)
                o_t.append(dot(vg, e.astype(BF16)) * inv)
            for u in range(2):
                parts = [o_t[g][:HD, u * L:(u + 1) * L] for g in range(3)]
                last = [pltpu.roll(o_t[g][HD:, u * L:(u + 1) * L], 32 + 32 * g, 1) for g in range(3)]
                parts.append(jnp.where(lane16 < 32, last[0], jnp.where(lane16 < 64, last[1], last[2])))
                att[u].append(jnp.concatenate(parts, axis=0) * gate[u][t * C:(t + 1) * C])
        return [jnp.transpose(jnp.concatenate(att[u], axis=0))[:NB] for u in range(2)]

    def g_copy(q):
        return pltpu.make_async_remote_copy(
            src_ref=g_send.at[pl.ds(q * CHUNK, CHUNK)], dst_ref=g_recv.at[pl.ds(q * CHUNK, CHUNK)],
            send_sem=g_ssem.at[q], recv_sem=g_rsem.at[q], device_id={"row": partner}, device_id_type=MESH)

    @pl.loop(0, NCH)
    def _(q):
        for slot, r in enumerate(peers):
            a_wait_recv(slot, q, r)

        @pl.loop(0, CHUNK)
        def _(i):
            p = q * CHUNK + i
            r0, r1 = pair(p)
            gf[pl.ds(s * 48 + p, NB, stride=NB), :] = jnp.where(s == 0, r0, r1)
            g_send[p] = jnp.where(s == 0, r1, r0).astype(BF16)

        g_copy(q).start()

    for q in range(NCH):
        g_copy(q).wait_recv()

    @pl.loop(0, PAIRS, unroll=2)
    def _(p):
        gf[pl.ds((1 - s) * 48 + p, NB, stride=NB), :] = g_recv[p].astype(F32)

    lane_o = lax.rem(lax.broadcasted_iota(jnp.int32, (C, NB), 1), 48)

    @pl.loop(0, NB, unroll=4)
    def _(i):
        gi = gf[pl.ds(pl.multiple_of(i * NB, NB), NB), :].astype(BF16)
        r = dot(wo2[...], gi, 1, 1)
        shifted = jnp.concatenate([jnp.zeros((C, PAIRS), F32), r[C:, :NB - PAIRS]], axis=1)
        upd = jnp.where(lane_o < PAIRS, r[:C], shifted)
        out_ref[i] = (z_ref[i].astype(F32) + upd).astype(BF16)

    for q in range(NCH):
        g_copy(q).wait_send()
        for slot, r in enumerate(peers):
            a_copy(slot, q, r).wait_send()

    @pl.when(jnp.logical_not(is_src))
    def _():
        bias_copy(b_own, u_own, row, b1_ssem, {"row": across}).wait_send()

    for u in range(2):
        for i in range(2):
            @pl.when(sends_right(u))
            def _(u=u, i=i):
                right(u, i).wait_send()

            @pl.when(sends_left(u))
            def _(u=u, i=i):
                left(u, i).wait_send()

            to_partner(u, i).wait_send()


def solution(mesh):
    vm = pl.BlockSpec(memory_space=pltpu.VMEM)
    dma = pltpu.SemaphoreType.DMA

    def body(pair_tile, res_mask, ln_gamma, ln_beta, w_q, w_k, w_v, w_b, w_g, w_o):
        out = pl.pallas_call(
            kernel,
            out_shape=jax.ShapeDtypeStruct((NB, C, NB), BF16),
            in_specs=[vm] * 10,
            out_specs=vm,
            scratch_shapes=[
                pltpu.VMEM((NB * 2 * PAIRS, L), F32),
                pltpu.VMEM((NB, 8, L), F32),
                pltpu.VMEM((2 * PAIRS, NB, L), BF16),
                pltpu.VMEM((PAIRS, NK + 32, L), BF16),
                pltpu.VMEM((3, NB, L), BF16),
                pltpu.VMEM((2, 4, 3, NB, L), BF16),
                pltpu.VMEM((2, 3, NK, L), F32),
                pltpu.VMEM((2, L, 6 * L), BF16),
                pltpu.VMEM((PAIRS, NB, L), BF16),
                pltpu.VMEM((PAIRS, NB, L), BF16),
                pltpu.VMEM((NB * NB, L), F32),
                pltpu.VMEM((L, L), BF16),
                pltpu.VMEM((L, L), BF16),
                pltpu.VMEM((2 * L, L), BF16),
                pltpu.VMEM((L, L), BF16),
                dma((3, NCH)), dma((3, NCH)), dma(()), dma((2, 2, 2)), dma((2, 4)), dma((2, 2)),
                dma((NCH,)), dma((NCH,)),
            ],
            compiler_params=pltpu.CompilerParams(collective_id=0, has_side_effects=True, vmem_limit_bytes=56 * 2**20),
            name="attend",
        )(jnp.transpose(pair_tile, (0, 2, 1)), res_mask, ln_gamma, ln_beta, w_q, w_k, w_v, w_b.T, w_g, w_o)
        return jnp.transpose(out, (0, 2, 1))

    tile_spec = P(("data", "row"), "col", None)
    return jax.shard_map(body, mesh=mesh, in_specs=(tile_spec, P("data"), P(), P(), P(), P(), P(), P(), P(), P()),
                         out_specs=tile_spec, check_vma=False)
```

time: 84.5 us -> 106 us (1.25)
  the two profiles are of different devices: /device:TPU:27 before, /device:TPU:4 now
where the time goes in v2:
time: 106 us; the launch traced here: 105 us
  Pallas kernels  103 us (97%)
  local copies, waits for them, and re-layouts  2.67 us (3%)
    pallas_call x1, Pallas kernels, body(): pl.pallas_call(kernel, out_shape=jax.ShapeDtypeStruct((NB, C, NB), BF16),...  103 us
    unnamed x1, local copies, waits for them, and re-layouts  2.67 us

profile of v2, /device:TPU:4, one launch (start us, length us, event | category | flops | bytes accessed | tf_op | source)
XLA Modules:
  0.0 105.5 jit_solution(472805591541519112)
XLA Ops:
  0.0 102.8 %attend.1 = bf16[96,64,96]{2,1,0:T(8,128)(2,1)} custom-call(bf16[96,64,96]{2,1,0:T(8,128)(2,1)} %bitcast.4, s32[384]{0:T(512)} %mask_ref.1, f32[64]{0:T(128)} %gam_ref.1, f32[64]{0:T(128)} %bet_ref.1, bf16[64,64]{1,0:T(8,128)(2,1)} %wq_ref.1, bf16[64,64]{1,0:T(8,128)(2,1)} %wk_ref.1, bf16[64,64]{1,0:T(8,128)(2,1)} %wv_ref.1, bf16[4,64]{1,0:T(4,128)(2,1)} %bitcast.5, ...), custom_call_target="tpu_custom_call" | custom-call | tf_op jit(solution)/shard_map/attend/pallas_call | solution.py:294
  102.8 2.7 %copy.12 = bf16[96,96,64]{1,2,0:T(8,128)(2,1)} copy(bf16[96,96,64]{1,2,0:T(8,128)(2,1)} %bitcast.3) | data formatting | bytes 2359296

commit v3 on v0

v3 whole, which is shorter than its diff:
```python
import math

import jax
import jax.numpy as jnp
from jax import lax
from jax.experimental import pallas as pl
from jax.experimental.pallas import tpu as pltpu
from jax.sharding import PartitionSpec as P

LN_EPS = 1e-5
MASK_FILL = -1e9
LOG2E = math.log2(math.e)
HEADS = 4
HD = 16
C = 64
NB = 96
NK = 384
NQ = 192
PAIRS = 24
CHUNK = 4
NCH = PAIRS // CHUNK
AHEAD = 2
L = 128
MESH = pl.DeviceIdType.MESH
F32 = jnp.float32
BF16 = jnp.bfloat16


def dot(a, b, ca=1, cb=0):
    return lax.dot_general(a, b, (((ca,), (cb,)), ((), ())), preferred_element_type=F32)


def blockdiag2(w):
    z = jnp.zeros_like(w)
    return jnp.concatenate([jnp.concatenate([w, z], 1), jnp.concatenate([z, w], 1)], 0)


def transposed(w):
    return jnp.transpose(w.astype(F32)).astype(BF16)


def down(v, n):
    return jnp.transpose(jnp.broadcast_to(v.reshape(1, n), (L, n)))


def kernel(z_ref, mask_ref, gam_ref, bet_ref, wq_ref, wk_ref, wv_ref, wbt_ref, wg_ref, wo_ref, out_ref,
           t_sc, b_sc, a_nat, a_own, a_all, bias_z, bias_in, bias_f, kbd, vbd, q_sc, gate_sc, p_sc, g_send, g_recv, gf,
           wk2, wv2, wqg2, wo2,
           a_ssem, a_rsem, z_ssem, z_rsem, y_ssem, f_ssem, b_rsem, g_ssem, g_rsem):
    col = lax.axis_index("col")
    row = lax.axis_index("row")
    y, s = row // 2, lax.rem(row, 2)
    partner = y * 2 + (1 - s)
    across = (1 - y) * 2 + s
    cross = (1 - y) * 2 + (1 - s)
    peers = (partner, across, cross)

    barrier = pltpu.get_barrier_semaphore()
    for r in peers:
        pl.semaphore_signal(barrier, inc=1, device_id={"row": r}, device_id_type=MESH)
    for d in range(1, 4):
        pl.semaphore_signal(barrier, inc=1, device_id={"col": lax.rem(col + d, 4)}, device_id_type=MESH)

    gam = down(gam_ref[...], C)[:, :NB]
    bet = down(bet_ref[...], C)[:, :NB]
    wbt = wbt_ref[...]

    @pl.loop(0, NB, unroll=4)
    def _(i):
        z = z_ref[i].astype(F32)
        mean = jnp.sum(z, axis=0, keepdims=True) * (1.0 / C)
        cen = z - mean
        var = jnp.sum(cen * cen, axis=0, keepdims=True) * (1.0 / C)
        a = cen * lax.rsqrt(var + LN_EPS) * gam + bet
        a_nat[i] = a.astype(BF16)
        b_sc[i, :HEADS, :NB] = dot(wbt, a.astype(BF16))

    lane = lax.broadcasted_iota(jnp.int32, (NB, L), 1)
    bh = [b_sc.reshape(NB * 8, L)[pl.ds(h, NB, stride=8), :] for h in range(HEADS)]
    for g in range(3):
        bias_z[col, g] = jnp.where(lane < NB, bh[g], pltpu.roll(bh[3], NB - 32 * g, 1)).astype(BF16)

    pl.semaphore_wait(barrier, 6)

    def z_copy(d):
        return pltpu.make_async_remote_copy(
            src_ref=bias_z.at[col], dst_ref=bias_z.at[col], send_sem=z_ssem.at[d], recv_sem=z_rsem.at[col],
            device_id={"col": lax.rem(col + 1 + d, 4)}, device_id_type=MESH)

    def z_wait(c):
        pltpu.make_async_remote_copy(
            src_ref=bias_z.at[c], dst_ref=bias_z.at[c], send_sem=z_ssem.at[0], recv_sem=z_rsem.at[c],
            device_id={"col": lax.rem(col + 1, 4)}, device_id_type=MESH).wait_recv()

    def bias_copy(src, u, r, ssem, dev):
        return pltpu.make_async_remote_copy(
            src_ref=src, dst_ref=bias_in.at[u, r], send_sem=ssem, recv_sem=b_rsem.at[u, r],
            device_id={"row": dev}, device_id_type=MESH)

    def y_copy(u):
        return bias_copy(bias_z.at[2 * (1 - y) + u], u, row, y_ssem.at[u], across)

    def own_copy(u):
        return bias_copy(bias_z.at[2 * y + u], u, row, f_ssem.at[u, 0], partner)

    def fwd_copy(u):
        return bias_copy(bias_in.at[u, across], u, across, f_ssem.at[u, 1], partner)

    def bias_wait(u, r):
        bias_copy(bias_in.at[u, r], u, r, y_ssem.at[u], partner).wait_recv()

    for d in range(3):
        z_copy(d).start()

    @pl.loop(0, NB, unroll=4)
    def _(i):
        at = jnp.transpose(a_nat[i].astype(F32))
        for half in range(2):
            o = half * 48
            t_sc[pl.ds(pl.multiple_of(i * 48 + half * PAIRS, 8), PAIRS), :] = jnp.concatenate(
                [at[o:o + PAIRS], at[o + PAIRS:o + 2 * PAIRS]], axis=1)

    @pl.loop(0, 2 * PAIRS, unroll=4)
    def _(n):
        a_own[n] = t_sc[pl.ds(n, NB, stride=2 * PAIRS), :].astype(BF16).reshape(3, 32, L)

    def a_desc(slot, q, r, last):
        dst = a_all.at[pl.ds(q * CHUNK, CHUNK), :, 3] if last else a_all.at[pl.ds(q * CHUNK, CHUNK), jnp.minimum(row, 2), 0:3]
        return pltpu.make_async_remote_copy(
            src_ref=a_own.at[pl.ds(lax.rem(r, 2) * PAIRS + q * CHUNK, CHUNK)], dst_ref=dst,
            send_sem=a_ssem.at[slot, q], recv_sem=a_rsem.at[slot, q],
            device_id={"row": r}, device_id_type=MESH)

    def a_start(slot, q):
        @pl.when(row == 3)
        def _():
            a_desc(slot, q, peers[slot], True).start()

        @pl.when(row < 3)
        def _():
            a_desc(slot, q, peers[slot], False).start()

    for q in range(AHEAD):
        for slot in (1, 2, 0):
            a_start(slot, q)

    @pl.when(row == 3)
    def _():
        a_all[:, :, 3] = a_own[pl.ds(s * PAIRS, PAIRS)]

    @pl.when(row < 3)
    def _():
        a_all[:, jnp.minimum(row, 2), 0:3] = a_own[pl.ds(s * PAIRS, PAIRS)]

    wk2[...] = blockdiag2(transposed(wk_ref[...]))
    wv2[...] = blockdiag2(wv_ref[...])
    wqg2[:, :L] = blockdiag2(wq_ref[...])
    wqg2[:, L:] = blockdiag2(wg_ref[...])
    wo2[...] = blockdiag2(wo_ref[...])
    for par in range(2):
        for t in range(2):
            kbd[par, t] = jnp.zeros((C, HEADS * NK), BF16)

    for u in range(2):
        @pl.when(2 * (1 - y) + u != col)
        def _(u=u):
            z_wait(2 * (1 - y) + u)
        y_copy(u).start()
    for q in range(AHEAD, NCH):
        for slot in (1, 2, 0):
            a_start(slot, q)
    for u in range(2):
        @pl.when(2 * y + u != col)
        def _(u=u):
            z_wait(2 * y + u)
        own_copy(u).start()
        bias_in[u, row] = bias_z[2 * y + u]
    for u in range(2):
        bias_wait(u, across)
        fwd_copy(u).start()
    for u in range(2):
        for r in (partner, cross):
            bias_wait(u, r)

    fill = down(jnp.where(mask_ref[...] > 0, 0.0, MASK_FILL).astype(F32), NK)
    for u in range(2):
        for g in range(3):
            parts = []
            for t in range(3):
                parts.append(bias_in[u, t, g].astype(F32) + fill[t * NB:(t + 1) * NB])
                parts.append(bias_in[u, 3, g, t * 32:(t + 1) * 32].astype(F32) + fill[3 * NB + t * 32:3 * NB + (t + 1) * 32])
            bt = jnp.transpose(jnp.concatenate(parts, axis=0)) * LOG2E
            bias_f[g, u * NB:(u + 1) * NB, :] = bt[:NB]
            bias_f[3, u * NB + g * 32:u * NB + (g + 1) * 32, :] = bt[NB:]

    hid = lax.broadcasted_iota(jnp.int32, (NK, C), 1) // HD
    hid_q = lax.broadcasted_iota(jnp.int32, (NQ, C), 1) // HD

    def project(p, par):
        x = a_all[p].reshape(NK, L)
        x_lo = a_all[p, 0:2, 0:3].reshape(NQ, L)
        x_hi = jnp.concatenate([a_all[p, 2, 0:3].reshape(NB, L), a_all[p, :, 3].reshape(NB, L)], axis=0)
        qg = dot(jnp.where(y == 0, x_lo, x_hi), wqg2[...])
        v2 = dot(x, wv2[...]).astype(BF16)
        kt = dot(wk2[...], x, 1, 1).astype(BF16)
        gate_sc[par] = jax.nn.sigmoid(qg[:, L:])
        for t in range(2):
            q_sc[par, t] = (qg[:, t * C:(t + 1) * C] * (1.0 / math.sqrt(HD))).astype(BF16)
            v_t = v2[:, t * C:(t + 1) * C]
            for h in range(HEADS):
                kbd[par, t, h * HD:(h + 1) * HD, h * NK:(h + 1) * NK] = kt[t * C + h * HD:t * C + (h + 1) * HD, :]
                vbd[par, t, h * NK:(h + 1) * NK, :] = jnp.where(hid == h, v_t, jnp.zeros_like(v_t))

    def attend(p, par):
        gated = []
        for t in range(2):
            inv = []
            for hp in range(2):
                logits = dot(q_sc[par, t], kbd[par, t, :, hp * 2 * NK:(hp + 1) * 2 * NK])
                for hh in range(2):
                    h = hp * 2 + hh
                    lt = logits[:, hh * NK:(hh + 1) * NK] * LOG2E + bias_f[h]
                    e = jnp.exp2(lt - jnp.max(lt, axis=1, keepdims=True))
                    inv.append(1.0 / jnp.sum(e, axis=1, keepdims=True))
                    p_sc[t, :, h * NK:(h + 1) * NK] = e.astype(BF16)
            o = dot(p_sc[t], vbd[par, t])
            scale = jnp.where(hid_q == 0, inv[0], jnp.where(hid_q == 1, inv[1], jnp.where(hid_q == 2, inv[2], inv[3])))
            gated.append(gate_sc[par, :, t * C:(t + 1) * C] * (o * scale))
        res = jnp.concatenate(gated, axis=1)
        gf[pl.ds(s * PAIRS + p, NB, stride=2 * PAIRS), :] = jnp.where(s == 0, res[:NB], res[NB:])
        g_send[p] = jnp.where(s == 0, res[NB:], res[:NB]).astype(BF16)

    def g_copy(q):
        return pltpu.make_async_remote_copy(
            src_ref=g_send.at[pl.ds(q * CHUNK, CHUNK)], dst_ref=g_recv.at[pl.ds(q * CHUNK, CHUNK)],
            send_sem=g_ssem.at[q], recv_sem=g_rsem.at[q], device_id={"row": partner}, device_id_type=MESH)

    def a_wait(q):
        for slot in range(3):
            a_desc(slot, q, peers[slot], False).wait_recv()

    a_wait(0)
    project(0, 0)

    @pl.loop(0, NCH)
    def _(q):
        @pl.loop(0, CHUNK // 2)
        def _(i):
            p = q * CHUNK + 2 * i

            @pl.when(jnp.logical_and(i == CHUNK // 2 - 1, q < NCH - 1))
            def _():
                a_wait(q + 1)

            project(p + 1, 1)
            attend(p, 0)
            project(jnp.minimum(p + 2, PAIRS - 1), 0)
            attend(p + 1, 1)

        g_copy(q).start()

    for q in range(NCH):
        g_copy(q).wait_recv()

    @pl.loop(0, PAIRS, unroll=4)
    def _(p):
        gf[pl.ds((1 - s) * PAIRS + p, NB, stride=2 * PAIRS), :] = g_recv[p].astype(F32)

    @pl.loop(0, NB // 4, unroll=2)
    def _(i4):
        r4 = dot(gf[pl.ds(pl.multiple_of(i4 * 192, 8), 192), :].astype(BF16), wo2[...])
        for k in range(4):
            r = r4[k * 48:(k + 1) * 48]
            rr = pltpu.roll(r, C, 1)
            jc = jnp.concatenate([r[:PAIRS], rr[:PAIRS], r[PAIRS:], rr[PAIRS:]], axis=0)
            i = i4 * 4 + k
            out_ref[i] = (z_ref[i].astype(F32) + jnp.transpose(jc)[:C]).astype(BF16)

    for q in range(NCH):
        g_copy(q).wait_send()
        for slot in range(3):
            a_desc(slot, q, peers[slot], False).wait_send()
    for d in range(3):
        z_copy(d).wait_send()
    for u in range(2):
        y_copy(u).wait_send()
        own_copy(u).wait_send()
        fwd_copy(u).wait_send()


def solution(mesh):
    vm = pl.BlockSpec(memory_space=pltpu.VMEM)
    dma = pltpu.SemaphoreType.DMA

    def body(pair_tile, res_mask, ln_gamma, ln_beta, w_q, w_k, w_v, w_b, w_g, w_o):
        out = pl.pallas_call(
            kernel,
            out_shape=jax.ShapeDtypeStruct((NB, C, NB), BF16),
            in_specs=[vm] * 10,
            out_specs=vm,
            scratch_shapes=[
                pltpu.VMEM((NB * 2 * PAIRS, L), F32),
                pltpu.VMEM((NB, 8, L), F32),
                pltpu.VMEM((NB, C, NB), BF16),
                pltpu.VMEM((2 * PAIRS, 3, 32, L), BF16),
                pltpu.VMEM((PAIRS, 3, 4, 32, L), BF16),
                pltpu.VMEM((4, 3, NB, L), BF16),
                pltpu.VMEM((2, 4, 3, NB, L), BF16),
                pltpu.VMEM((HEADS, NQ, NK), F32),
                pltpu.VMEM((2, 2, C, HEADS * NK), BF16),
                pltpu.VMEM((2, 2, HEADS * NK, C), BF16),
                pltpu.VMEM((2, 2, NQ, C), BF16),
                pltpu.VMEM((2, NQ, L), F32),
                pltpu.VMEM((2, NQ, HEADS * NK), BF16),
                pltpu.VMEM((PAIRS, NB, L), BF16),
                pltpu.VMEM((PAIRS, NB, L), BF16),
                pltpu.VMEM((NB * 2 * PAIRS, L), F32),
                pltpu.VMEM((L, L), BF16),
                pltpu.VMEM((L, L), BF16),
                pltpu.VMEM((L, 2 * L), BF16),
                pltpu.VMEM((L, L), BF16),
                dma((3, NCH)), dma((3, NCH)), dma((3,)), dma((4,)), dma((2,)), dma((2, 2)), dma((2, 4)),
                dma((NCH,)), dma((NCH,)),
            ],
            compiler_params=pltpu.CompilerParams(collective_id=0, has_side_effects=True, vmem_limit_bytes=56 * 2**20),
            name="attend",
        )(jnp.transpose(pair_tile, (0, 2, 1)), res_mask, ln_gamma, ln_beta, w_q, w_k, w_v, w_b.T, w_g, w_o)
        return jnp.transpose(out, (0, 2, 1))

    tile_spec = P(("data", "row"), "col", None)
    return jax.shard_map(body, mesh=mesh, in_specs=(tile_spec, P("data"), P(), P(), P(), P(), P(), P(), P(), P()),
                         out_specs=tile_spec, check_vma=False)
```

time: 346 us -> 69.6 us (0.20); the launches traced: 342 us -> 69.5 us
  waiting for transfers between devices: 105 us -> 0 us
  matrix products: 84.5 us -> 0 us
  other arithmetic: 70.6 us -> 0 us
  Pallas kernels: 0 us -> 66.8 us
  local copies, waits for them, and re-layouts: 59.8 us -> 2.67 us
  blocking collectives: 16.3 us -> 0 us
  starting transfers between devices: 4.81 us -> 0 us
    ppermute x3 -> x0, waiting for transfers between devices: 105 us -> none  [shift_step(): kv_blk = lax.ppermute(kv_blk, 'row', next_hop)]
    dot_general x12 -> x0, matrix products: 84.5 us -> none  [the longest x4 39.6 us: attend_block(): jnp.einsum('jhid,jhkd->jhik', query, kv_blk[0], preferred_element_type=jn...]
    pallas_call x0 -> x1, Pallas kernels: none -> 66.8 us  [body(): pl.pallas_call(kernel, out_shape=jax.ShapeDtypeStruct((NB, C, NB), BF16),...]
    reduce_sum x6 -> x0, other arithmetic: 53.7 us -> none  [the longest x4 52.4 us: attend_block(): run_sum = run_sum * rescale + jnp.sum(p_exp, axis=-1)]
    while x31 -> x0, local copies, waits for them, and re-layouts: 22.6 us -> none
    all_gather x1 -> x0, blocking collectives: 16.3 us -> none  [bias_strip(): full_cols = lax.all_gather(bias_tile, 'col', axis=1, tiled=True)]
    convert_element_type x4 -> x0, local copies, waits for them, and re-layouts: 16.1 us -> none  [the longest x2 8.08 us: norm_and_project(): (centred * lax.rsqrt(variance + LN_EPS) * ln_gamma + ln_beta).astype(jnp....]
    squeeze x3 -> x0, local copies, waits for them, and re-layouts: 10.9 us -> none  [the longest x2 6.56 us: attend_block(): kv_blk[1]]
  transfers between devices with their start and end apart: 4 -> 0, of which waited for: 3 -> 0; matrix products, arithmetic and copies ran while one was open for 13% -> 0% of each run, Pallas kernels for 0% -> 0%
where the time goes in v3:
time: 69.6 us; the launch traced here: 69.5 us
  Pallas kernels  66.8 us (96%)
  local copies, waits for them, and re-layouts  2.67 us (4%)
    pallas_call x1, Pallas kernels, body(): pl.pallas_call(kernel, out_shape=jax.ShapeDtypeStruct((NB, C, NB), BF16),...  66.8 us
    unnamed x1, local copies, waits for them, and re-layouts  2.67 us

profile of v3, /device:TPU:0, one launch (start us, length us, event | category | flops | bytes accessed | tf_op | source)
XLA Modules:
  0.0 69.5 jit_solution(8242486235282398167)
XLA Ops:
  0.0 66.8 %attend.1 = bf16[96,64,96]{2,1,0:T(8,128)(2,1)} custom-call(bf16[96,64,96]{2,1,0:T(8,128)(2,1)} %bitcast.4, s32[384]{0:T(512)} %mask_ref.1, f32[64]{0:T(128)} %gam_ref.1, f32[64]{0:T(128)} %bet_ref.1, bf16[64,64]{1,0:T(8,128)(2,1)} %wq_ref.1, bf16[64,64]{1,0:T(8,128)(2,1)} %wk_ref.1, bf16[64,64]{1,0:T(8,128)(2,1)} %wv_ref.1, bf16[4,64]{1,0:T(4,128)(2,1)} %bitcast.5, ...), custom_call_target="tpu_custom_call" | custom-call | tf_op jit(solution)/shard_map/attend/pallas_call | solution.py:296
  66.8 2.7 %copy.12 = bf16[96,96,64]{1,2,0:T(8,128)(2,1)} copy(bf16[96,96,64]{1,2,0:T(8,128)(2,1)} %bitcast.3) | data formatting | bytes 2359296
